TPU v7x, 64 devices: a 2x2x8 block of a 4x4x8 slice. The times are simulated.
64 devices in a mesh: rep: 8 (over x, y, core), dp: 8 (over z).
Axes of the slice: x: 2, y: 2, z: 8, core: 2. Of those that a mesh axis runs over, the one named last changes fastest.
The devices are a block of a 4x4x8 slice.
Arguments:
- g_w_gate: bfloat16 [64, 2, 512, 3072], P(('rep', 'dp')), parts along dimension 0
- g_w_up: bfloat16 [64, 2, 512, 3072], P(('rep', 'dp')), parts along dimension 0
- g_w_down: bfloat16 [64, 2, 3072, 512], P(('rep', 'dp')), parts along dimension 0
- w_gate: bfloat16 [2, 512, 3072], replicated
- w_up: bfloat16 [2, 512, 3072], replicated
- w_down: bfloat16 [2, 3072, 512], replicated
- m_w_gate: float32 [2, 512, 3072], P(None, 'dp')
- m_w_up: float32 [2, 512, 3072], P(None, 'dp')
- m_w_down: float32 [2, 3072, 512], P(None, 'dp')
- v_w_gate: float32 [2, 512, 3072], P(None, 'dp')
- v_w_up: float32 [2, 512, 3072], P(None, 'dp')
- v_w_down: float32 [2, 3072, 512], P(None, 'dp')
Outputs:
- output 1: bfloat16 [16, 512, 3072], P('rep'), parts along dimension 0
- output 2: bfloat16 [16, 512, 3072], P('rep'), parts along dimension 0
- output 3: bfloat16 [16, 3072, 512], P('rep'), parts along dimension 0
- output 4: float32 [16, 512, 3072], P('rep', 'dp'), parts along dimension 0
- output 5: float32 [16, 512, 3072], P('rep', 'dp'), parts along dimension 0
- output 6: float32 [16, 3072, 512], P('rep', 'dp'), parts along dimension 0
- output 7: float32 [16, 512, 3072], P('rep', 'dp'), parts along dimension 0
- output 8: float32 [16, 512, 3072], P('rep', 'dp'), parts along dimension 0
- output 9: float32 [16, 3072, 512], P('rep', 'dp'), parts along dimension 0
There are 8 independent parts. A program takes and returns all parts, laid end to end along the dimension named above; an argument that names none is the same for every part.
All inputs are finite; a program needn't handle non-finite values.
Results may differ from a plain program's by a relative error of at most 0.022.
Values are sent between devices in bfloat16 or wider.
A program may use at most 768 MiB of HBM per device.

v0:
```python
import functools

import jax
import jax.numpy as jnp
from jax import lax
from jax.experimental import pallas as pl
from jax.experimental.pallas import tpu as pltpu
from jax.sharding import PartitionSpec as P

MESH = pl.DeviceIdType.MESH
F32, BF16 = jnp.float32, jnp.bfloat16
ROWS, COLS = 16, 512
AHEAD = 3
LAG = 16000


def adamw(w, m, v, g):
    m = 0.9 * m + 0.1 * g
    v = 0.95 * v + 0.05 * g * g
    step = m * lax.rsqrt(v + 1e-8) + 0.1 * w
    return (w - 0.02 * step).astype(BF16), m, v


def tiles(shape, body):
    across = shape[1] // COLS

    @pl.loop(0, (shape[0] // ROWS) * across)
    def _(i):
        r = pl.multiple_of((i // across) * ROWS, ROWS)
        c = pl.multiple_of((i % across) * COLS, COLS)
        body(pl.ds(r, ROWS), pl.ds(c, COLS))


class Ring:
    def __init__(self, axis, n):
        self.axis, self.n = axis, n
        self.me = lax.axis_index(axis)
        self.target = (lax.rem(self.me + 1, n), lax.rem(self.me + n - 1, n))

    def greet(self):
        barrier = pltpu.get_barrier_semaphore()
        for neighbour in self.target:
            pl.semaphore_signal(barrier, inc=1, device_id={self.axis: neighbour}, device_id_type=MESH)
        pl.semaphore_wait(barrier, 2)

    def start_of(self, d, hops, rows):
        owner = lax.rem(self.me + (-1, 1)[d] * hops + 2 * self.n, self.n)
        return pl.multiple_of(owner * rows, rows)

    def copy(self, d, src, dst, send, recv):
        return pltpu.make_async_remote_copy(
            src_ref=src, dst_ref=dst, send_sem=send, recv_sem=recv,
            device_id={self.axis: self.target[d]}, device_id_type=MESH,
        )


def first_kernel(n, axis, groups, *refs):
    it = iter(refs)
    take = lambda k: [next(it) for _ in range(k)]
    g_hbm, w_hbm, m_hbm, v_hbm = take(3), take(3), take(3), take(3)
    w_out, m_out, v_out = take(3), take(3), take(3)
    slots, terms, own = take(3), take(3), take(3)
    rs_send, rs_recv, ag_send, ag_recv, term_sem, state_sem = take(6)

    ring = Ring(axis, n)
    rows = [w.shape[1] for w in own]
    pairs = [(q, d) for q in range(3) for d in range(2)]
    last = n - 2

    def block(d, hops, q):
        return pl.ds(ring.start_of(d, hops, rows[q]), rows[q])

    def rs_copy(q, d, s, src):
        return ring.copy(d, src, slots[q].at[d, s], rs_send.at[q, d, s], rs_recv.at[q, d, s])

    def ag_copy(q, d, s):
        ref = w_out[q].at[d, block(d, s, q)]
        return ring.copy(d, ref, ref, ag_send.at[q, d, s], ag_recv.at[q, d, s])

    def term_copy(q, d, s):
        slot = lax.rem(s, AHEAD)
        return pltpu.make_async_copy(g_hbm[q].at[d, block(d, s + 2, q)], terms[q].at[d, slot], term_sem.at[q, d, slot])

    def state_copies(q):
        return (
            pltpu.make_async_copy(w_hbm[q].at[:, block(0, 0, q)], own[q], state_sem.at[q, 0]),
            pltpu.make_async_copy(m_hbm[q], m_out[q], state_sem.at[q, 1]),
            pltpu.make_async_copy(v_hbm[q], v_out[q], state_sem.at[q, 2]),
        )

    ring.greet()
    if LAG:
        @pl.when(lax.rem(lax.axis_index(groups), 2) == 1)
        def _():
            pl.delay(LAG)

    for q, d in pairs:
        rs_copy(q, d, 0, g_hbm[q].at[d, block(d, 1, q)]).start()
    for s in range(AHEAD):
        for q, d in pairs:
            term_copy(q, d, s).start()
    for q in range(3):
        for c in state_copies(q):
            c.start()

    @pl.loop(0, last)
    def _(s):
        for q, d in pairs:
            slot = slots[q].at[d, s]
            term = terms[q].at[d, lax.rem(s, AHEAD)]
            rs_copy(q, d, s, slot).wait_recv()
            term_copy(q, d, s).wait()

            def add(r, c):
                slot[r, c] = (slot[r, c].astype(F32) + term[r, c].astype(F32)).astype(BF16)

            tiles(term.shape, add)
            rs_copy(q, d, s + 1, slot).start()

            @pl.when(s + AHEAD < n - 1)
            def _():
                term_copy(q, d, s + AHEAD).start()

    for q in range(3):
        for c in state_copies(q):
            c.wait()
    for q, d in pairs:
        slot, term = slots[q].at[d, last], terms[q].at[d, last % AHEAD]
        base = ring.start_of(0, 0, rows[q])
        rs_copy(q, d, last, slot).wait_recv()
        term_copy(q, d, last).wait()

        def update(r, c):
            g = (slot[r, c].astype(F32) + term[r, c].astype(F32)).astype(BF16).astype(F32)
            w, m, v = adamw(own[q][d, r, c].astype(F32), m_out[q][d, r, c], v_out[q][d, r, c], g)
            w_out[q][d, pl.ds(pl.multiple_of(base + r.start, ROWS), ROWS), c] = w
            m_out[q][d, r, c] = m
            v_out[q][d, r, c] = v

        tiles(term.shape, update)
        ag_copy(q, d, 0).start()

    @pl.loop(0, last - 1)
    def _(s):
        for q, d in pairs:
            ag_copy(q, d, s).wait_recv()
            ag_copy(q, d, s + 1).start()

    for q, d in pairs:
        ag_copy(q, d, last - 1).wait_recv()

    @pl.loop(0, last)
    def _(s):
        for q, d in pairs:
            rs_copy(q, d, s, slots[q].at[d, s]).wait_send()
            ag_copy(q, d, s).wait_send()

    for q, d in pairs:
        rs_copy(q, d, last, slots[q].at[d, last]).wait_send()


def second_kernel(n, axis, *refs):
    w, out, send, recv = refs[:3], refs[3:6], refs[6], refs[7]
    ring = Ring(axis, n)
    rows = [o.shape[1] for o in out]
    copies = [
        ring.copy(d, w[q].at[d, pl.ds(ring.start_of(d, n - 2, rows[q]), rows[q])], out[q].at[d], send.at[q, d], recv.at[q, d])
        for q in range(3)
        for d in range(2)
    ]
    ring.greet()
    for c in copies:
        c.start()
    for c in copies:
        c.wait()


def out_kernel(*refs):
    k = len(refs) // 2
    copies = [pltpu.make_async_copy(refs[i], refs[k + i], refs[-1].at[i]) for i in range(k)]
    for c in copies:
        c.start()
    for c in copies:
        c.wait()


def written(*arrays):
    return pl.pallas_call(
        out_kernel,
        out_shape=tuple(jax.ShapeDtypeStruct(a.shape, a.dtype) for a in arrays),
        in_specs=[pl.BlockSpec(memory_space=pltpu.VMEM)] * len(arrays),
        out_specs=tuple([pl.BlockSpec(memory_space=pltpu.HBM)] * len(arrays)),
        scratch_shapes=[pltpu.SemaphoreType.DMA((len(arrays),))],
        compiler_params=pltpu.CompilerParams(vmem_limit_bytes=2**20, has_side_effects=True),
    )(*arrays)


def last_kernel(n, axis, *refs):
    blocks, out, sem = refs[:3], refs[6:9], refs[9]
    ring = Ring(axis, n)
    copies = []
    for q in range(3):
        rows = blocks[q].shape[1]
        for d in range(2):
            there = out[q].at[d, pl.ds(ring.start_of(d, n - 1, rows), rows)]
            copies.append(pltpu.make_async_copy(blocks[q].at[d], there, sem.at[q, d]))
    for c in copies:
        c.start()
    for c in copies:
        c.wait()


def solution(mesh):
    groups, axis = "rep", "dp"
    n = mesh.shape[axis]
    dma = pltpu.SemaphoreType.DMA
    vmem, hbm = pl.BlockSpec(memory_space=pltpu.VMEM), pl.BlockSpec(memory_space=pltpu.HBM)

    def step(*arrays):
        terms, weights, m, v = (arrays[i : i + 3] for i in (0, 3, 6, 9))
        terms = [t[0] for t in terms]
        shares = [(one.shape[1], one.shape[2]) for one in m]
        whole = [pltpu.VMEM(w.shape, BF16) for w in weights]
        state = [pltpu.VMEM(one.shape, F32) for one in (*m, *v)]
        results = pl.pallas_call(
            functools.partial(first_kernel, n, axis, groups),
            out_shape=(*whole, *state),
            in_specs=[hbm] * 12,
            out_specs=tuple([vmem] * 9),
            scratch_shapes=[
                *[pltpu.VMEM((2, n - 1, *s), BF16) for s in shares],
                *[pltpu.VMEM((2, AHEAD, *s), BF16) for s in shares],
                *[pltpu.VMEM((2, *s), BF16) for s in shares],
                *[dma((3, 2, n - 1))] * 2,
                *[dma((3, 2, n - 2))] * 2,
                dma((3, 2, AHEAD)),
                dma((3, 3)),
            ],
            compiler_params=pltpu.CompilerParams(
                collective_id=0, has_side_effects=True, vmem_limit_bytes=30 * 2**20
            ),
        )(*terms, *weights, *m, *v)
        first = written(*results)
        gathered, first = lax.optimization_barrier((results[:3], first))
        blocks = pl.pallas_call(
            functools.partial(second_kernel, n, axis),
            out_shape=tuple(pltpu.VMEM((2, *s), BF16) for s in shares),
            in_specs=[vmem] * 3,
            out_specs=tuple([vmem] * 3),
            scratch_shapes=[dma((3, 2))] * 2,
            compiler_params=pltpu.CompilerParams(
                collective_id=1, has_side_effects=True, vmem_limit_bytes=2**20
            ),
        )(*gathered)
        complete = pl.pallas_call(
            functools.partial(last_kernel, n, axis),
            out_shape=tuple(jax.ShapeDtypeStruct(w.shape, BF16) for w in weights),
            in_specs=[vmem] * 3 + [hbm] * 3,
            out_specs=tuple([hbm] * 3),
            scratch_shapes=[dma((3, 2))],
            input_output_aliases={3: 0, 4: 1, 5: 2},
            compiler_params=pltpu.CompilerParams(vmem_limit_bytes=2**20, has_side_effects=True),
        )(*blocks, *first[:3])
        return (*complete, *first[3:])

    all_of, cut = P(None, None, None), P(None, "dp", None)
    return jax.shard_map(
        step,
        mesh=mesh,
        in_specs=(P(("rep", "dp"), None, None, None),) * 3 + (all_of,) * 3 + (cut,) * 6,
        out_specs=(P("rep", None, None),) * 3 + (P("rep", "dp", None),) * 6,
        check_vma=False,
    )
```

profile of v0, /device:TPU:21, one launch (start us, length us, event | category | flops | bytes accessed | tf_op | source)
XLA Modules:
  0.0 368.9 jit_solution(14367291682561280429)
XLA Ops:
  0.6 340.8 %shard_map.187 = (bf16[2,512,3072]{2,1,0:T(8,128)(2,1)S(1)}, bf16[2,512,3072]{2,1,0:T(8,128)(2,1)S(1)}, bf16[2,3072,512]{2,1,0:T(8,128)(2,1)S(1)}, f32[2,64,3072...) custom-call(bf16[2,512,3072]{2,1,0:T(8,128)(2,1)} %bitcast.3, ...), custom_call_target="tpu_custom_call" | custom-call | tf_op jit(solution)/shard_map/pallas_call | solution.py:225
  341.5 9.4 %shard_map.188 = (bf16[2,512,3072]{2,1,0:T(8,128)(2,1)}, bf16[2,512,3072]{2,1,0:T(8,128)(2,1)}, bf16[2,3072,512]{2,1,0:T(8,128)(2,1)}, f32[2,64,3072]{2,1,0:T(8,...) custom-call(bf16[2,512,3072]{2,1,0:T(8,128)(2,1)S(1)} %get-tuple-ele, ...), custom_call_target="tpu_custom_call" | custom-call | tf_op jit(solution)/shard_map/pallas_call | solution.py:188
  350.9 16.5 %shard_map.189 = (bf16[2,64,3072]{2,1,0:T(8,128)(2,1)S(1)}, bf16[2,64,3072]{2,1,0:T(8,128)(2,1)S(1)}, bf16[2,384,512]{2,1,0:T(8,128)(2,1)S(1)}) custom-call(bf16[2,512,3072]{2,1,0:T(8,128)(2,1)S(1)} %get-tuple-element.63.refs_0_, bf16[2,512,3072]{2,1,0:T(8,128)(2,1)S(1)} %get-tuple-element.64.refs_1_, bf16[2,3072,512]{2,1,0:T(8,128)(2,1)S(1)} %get-tuple-element.65.refs_2_), custom_call_target="tpu_custom_call" | custom-call | tf_op jit(solution)/shard_map/pallas_call | solution.py:245
  367.4 1.5 shard_map.190
where the time goes:
time: 369 us
  Pallas kernels  368 us (100%)
    pallas_call x1, Pallas kernels, step(): pl.pallas_call(functools.partial(first_kernel, n, axis, groups), out_shap...  341 us
    pallas_call x1, Pallas kernels, step(): pl.pallas_call(functools.partial(second_kernel, n, axis), out_shape=tuple...  16.5 us
    pallas_call x1, Pallas kernels, written(): pl.pallas_call(out_kernel, out_shape=tuple((jax.ShapeDtypeStruct(a.shape,...  9.45 us

commit v1 on v0

--- a/solution.py
+++ b/solution.py
@@ -11,7 +11,8 @@
 F32, BF16 = jnp.float32, jnp.bfloat16
 ROWS, COLS = 16, 512
 AHEAD = 3
-LAG = 16000
+LATE = (1, 1, 2)
+LAG = 18000
 
 
 def adamw(w, m, v, g):
@@ -99,12 +100,15 @@
     for s in range(AHEAD):
         for q, d in pairs:
             term_copy(q, d, s).start()
-    for q in range(3):
-        for c in state_copies(q):
-            c.start()
 
     @pl.loop(0, last)
     def _(s):
+        @pl.when(s == 1)
+        def _():
+            for q in range(3):
+                for c in state_copies(q):
+                    c.start()
+
         for q, d in pairs:
             slot = slots[q].at[d, s]
             term = terms[q].at[d, lax.rem(s, AHEAD)]
@@ -120,6 +124,10 @@
             @pl.when(s + AHEAD < n - 1)
             def _():
                 term_copy(q, d, s + AHEAD).start()
+
+            @pl.when(s > 0)
+            def _():
+                rs_copy(q, d, s - 1, slots[q].at[d, s - 1]).wait_send()
 
     for q in range(3):
         for c in state_copies(q):
@@ -140,39 +148,55 @@
         tiles(term.shape, update)
         ag_copy(q, d, 0).start()
 
-    @pl.loop(0, last - 1)
+    steps = [n - 1 - k for k in LATE]
+
+    @pl.loop(0, min(steps) - 1)
     def _(s):
         for q, d in pairs:
             ag_copy(q, d, s).wait_recv()
             ag_copy(q, d, s + 1).start()
 
+            @pl.when(s > 0)
+            def _():
+                ag_copy(q, d, s - 1).wait_send()
+
+            @pl.when(s < 2)
+            def _():
+                rs_copy(q, d, last - 1 + s, slots[q].at[d, last]).wait_send()
+
+    for s in range(min(steps) - 1, max(steps)):
+        for q, d in pairs:
+            if s < steps[q]:
+                ag_copy(q, d, s).wait_recv()
+            if s + 1 < steps[q]:
+                ag_copy(q, d, s + 1).start()
     for q, d in pairs:
-        ag_copy(q, d, last - 1).wait_recv()
-
-    @pl.loop(0, last)
-    def _(s):
-        for q, d in pairs:
-            rs_copy(q, d, s, slots[q].at[d, s]).wait_send()
+        for s in range(min(steps) - 2, steps[q]):
             ag_copy(q, d, s).wait_send()
-
-    for q, d in pairs:
-        rs_copy(q, d, last, slots[q].at[d, last]).wait_send()
 
 
 def second_kernel(n, axis, *refs):
     w, out, send, recv = refs[:3], refs[3:6], refs[6], refs[7]
     ring = Ring(axis, n)
-    rows = [o.shape[1] for o in out]
-    copies = [
-        ring.copy(d, w[q].at[d, pl.ds(ring.start_of(d, n - 2, rows[q]), rows[q])], out[q].at[d], send.at[q, d], recv.at[q, d])
-        for q in range(3)
-        for d in range(2)
-    ]
+
+    def copy(q, d, j):
+        rows = out[q].shape[2]
+        src = out[q].at[d, j - 1] if j else w[q].at[d, pl.ds(ring.start_of(d, n - 1 - LATE[q], rows), rows)]
+        return ring.copy(d, src, out[q].at[d, j], send.at[q, d, j], recv.at[q, d, j])
+
     ring.greet()
-    for c in copies:
-        c.start()
-    for c in copies:
-        c.wait()
+    for j in range(max(LATE)):
+        for q in sorted(range(3), key=lambda q: -LATE[q]):
+            for d in range(2):
+                if j < LATE[q]:
+                    if j:
+                        copy(q, d, j - 1).wait_recv()
+                    copy(q, d, j).start()
+    for q in range(3):
+        for d in range(2):
+            for j in range(LATE[q]):
+                copy(q, d, j).wait_send()
+            copy(q, d, LATE[q] - 1).wait_recv()
 
 
 def out_kernel(*refs):
@@ -200,10 +224,11 @@
     ring = Ring(axis, n)
     copies = []
     for q in range(3):
-        rows = blocks[q].shape[1]
+        rows = blocks[q].shape[2]
         for d in range(2):
-            there = out[q].at[d, pl.ds(ring.start_of(d, n - 1, rows), rows)]
-            copies.append(pltpu.make_async_copy(blocks[q].at[d], there, sem.at[q, d]))
+            for j in range(LATE[q]):
+                there = out[q].at[d, pl.ds(ring.start_of(d, n - LATE[q] + j, rows), rows)]
+                copies.append(pltpu.make_async_copy(blocks[q].at[d, j], there, sem.at[q, d, j]))
     for c in copies:
         c.start()
     for c in copies:
@@ -231,8 +256,7 @@
                 *[pltpu.VMEM((2, n - 1, *s), BF16) for s in shares],
                 *[pltpu.VMEM((2, AHEAD, *s), BF16) for s in shares],
                 *[pltpu.VMEM((2, *s), BF16) for s in shares],
-                *[dma((3, 2, n - 1))] * 2,
-                *[dma((3, 2, n - 2))] * 2,
+                *[dma((3, 2, n - 1))] * 4,
                 dma((3, 2, AHEAD)),
                 dma((3, 3)),
             ],
@@ -244,10 +268,10 @@
         gathered, first = lax.optimization_barrier((results[:3], first))
         blocks = pl.pallas_call(
             functools.partial(second_kernel, n, axis),
-            out_shape=tuple(pltpu.VMEM((2, *s), BF16) for s in shares),
+            out_shape=tuple(pltpu.VMEM((2, k, *s), BF16) for k, s in zip(LATE, shares, strict=True)),
             in_specs=[vmem] * 3,
             out_specs=tuple([vmem] * 3),
-            scratch_shapes=[dma((3, 2))] * 2,
+            scratch_shapes=[dma((3, 2, max(LATE)))] * 2,
             compiler_params=pltpu.CompilerParams(
                 collective_id=1, has_side_effects=True, vmem_limit_bytes=2**20
             ),
@@ -257,7 +281,7 @@
             out_shape=tuple(jax.ShapeDtypeStruct(w.shape, BF16) for w in weights),
             in_specs=[vmem] * 3 + [hbm] * 3,
             out_specs=tuple([hbm] * 3),
-            scratch_shapes=[dma((3, 2))],
+            scratch_shapes=[dma((3, 2, max(LATE)))],
             input_output_aliases={3: 0, 4: 1, 5: 2},
             compiler_params=pltpu.CompilerParams(vmem_limit_bytes=2**20, has_side_effects=True),
         )(*blocks, *first[:3])

time: 369 us -> 367 us (level)
    pallas_call x1, Pallas kernels: 341 us -> 334 us  [step(): pl.pallas_call(functools.partial(first_kernel, n, axis, groups), out_shap...]
    pallas_call x1, Pallas kernels: 16.5 us -> 21.6 us  [step(): pl.pallas_call(functools.partial(second_kernel, n, axis), out_shape=tuple...]
where the time goes in v1:
time: 367 us
  Pallas kernels  366 us (100%)
    pallas_call x1, Pallas kernels, step(): pl.pallas_call(functools.partial(first_kernel, n, axis, groups), out_shap...  334 us
    pallas_call x1, Pallas kernels, step(): pl.pallas_call(functools.partial(second_kernel, n, axis), out_shape=tuple...  21.6 us
    pallas_call x1, Pallas kernels, written(): pl.pallas_call(out_kernel, out_shape=tuple((jax.ShapeDtypeStruct(a.shape,...  9.45 us

profile of v1, /device:TPU:21, one launch (start us, length us, event | category | flops | bytes accessed | tf_op | source)
XLA Modules:
  0.0 367.0 jit_solution(1156388155051819160)
XLA Ops:
  0.6 333.5 %shard_map.187 = (bf16[2,512,3072]{2,1,0:T(8,128)(2,1)S(1)}, bf16[2,512,3072]{2,1,0:T(8,128)(2,1)S(1)}, bf16[2,3072,512]{2,1,0:T(8,128)(2,1)S(1)}, f32[2,64,3072...) custom-call(bf16[2,512,3072]{2,1,0:T(8,128)(2,1)} %bitcast.3, ...), custom_call_target="tpu_custom_call" | custom-call | tf_op jit(solution)/shard_map/pallas_call | solution.py:250
  334.2 9.4 %shard_map.188 = (bf16[2,512,3072]{2,1,0:T(8,128)(2,1)}, bf16[2,512,3072]{2,1,0:T(8,128)(2,1)}, bf16[2,3072,512]{2,1,0:T(8,128)(2,1)}, f32[2,64,3072]{2,1,0:T(8,...) custom-call(bf16[2,512,3072]{2,1,0:T(8,128)(2,1)S(1)} %get-tuple-ele, ...), custom_call_target="tpu_custom_call" | custom-call | tf_op jit(solution)/shard_map/pallas_call | solution.py:212
  343.7 21.6 %shard_map.189 = (bf16[2,1,64,3072]{3,2,1,0:T(8,128)(2,1)S(1)}, bf16[2,1,64,3072]{3,2,1,0:T(8,128)(2,1)S(1)}, bf16[2,2,384,512]{3,2,1,0:T(8,128)(2,1)S(1)}) custom-call(bf16[2,512,3072]{2,1,0:T(8,128)(2,1)S(1)} %get-tuple-element.63.refs_0_, bf16[2,512,3072]{2,1,0:T(8,128)(2,1)S(1)} %get-tuple-element.64.refs_1_, ...), custom_call_target="tpu_custom_call" | custom-call | tf_op jit(solution)/shard_map/pallas_call | solution.py:269
  365.2 1.8 shard_map.190

commit v2 on v1

--- a/solution.py
+++ b/solution.py
@@ -12,7 +12,7 @@
 ROWS, COLS = 16, 512
 AHEAD = 3
 LATE = (1, 1, 2)
-LAG = 18000
+LAG = 5000
 
 
 def adamw(w, m, v, g):
@@ -20,6 +20,10 @@
     v = 0.95 * v + 0.05 * g * g
     step = m * lax.rsqrt(v + 1e-8) + 0.1 * w
     return (w - 0.02 * step).astype(BF16), m, v
+
+
+def is_odd(groups):
+    return lax.rem(lax.axis_index(groups), 2) == 1
 
 
 def tiles(shape, body):
@@ -67,6 +71,7 @@
     rows = [w.shape[1] for w in own]
     pairs = [(q, d) for q in range(3) for d in range(2)]
     last = n - 2
+    odd = is_odd(groups)
 
     def block(d, hops, q):
         return pl.ds(ring.start_of(d, hops, rows[q]), rows[q])
@@ -91,9 +96,7 @@
 
     ring.greet()
     if LAG:
-        @pl.when(lax.rem(lax.axis_index(groups), 2) == 1)
-        def _():
-            pl.delay(LAG)
+        pl.when(odd)(lambda: pl.delay(LAG))
 
     for q, d in pairs:
         rs_copy(q, d, 0, g_hbm[q].at[d, block(d, 1, q)]).start()
@@ -170,33 +173,47 @@
                 ag_copy(q, d, s).wait_recv()
             if s + 1 < steps[q]:
                 ag_copy(q, d, s + 1).start()
+            elif s + 1 == steps[q]:
+                pl.when(odd)(lambda: ag_copy(q, d, s + 1).start())
     for q, d in pairs:
         for s in range(min(steps) - 2, steps[q]):
             ag_copy(q, d, s).wait_send()
 
-
-def second_kernel(n, axis, *refs):
+    @pl.when(odd)
+    def _():
+        for q, d in pairs:
+            ag_copy(q, d, steps[q]).wait()
+
+
+def second_kernel(n, axis, groups, *refs):
     w, out, send, recv = refs[:3], refs[3:6], refs[6], refs[7]
     ring = Ring(axis, n)
-
-    def copy(q, d, j):
+    odd = is_odd(groups)
+
+    def copy(q, d, j, first):
         rows = out[q].shape[2]
-        src = out[q].at[d, j - 1] if j else w[q].at[d, pl.ds(ring.start_of(d, n - 1 - LATE[q], rows), rows)]
+        hops = n - 1 - LATE[q] + j
+        src = w[q].at[d, pl.ds(ring.start_of(d, hops, rows), rows)] if j == first else out[q].at[d, j - 1]
         return ring.copy(d, src, out[q].at[d, j], send.at[q, d, j], recv.at[q, d, j])
 
+    def gather(first):
+        for j in range(first, max(LATE)):
+            for q in sorted(range(3), key=lambda q: -LATE[q]):
+                for d in range(2):
+                    if j < LATE[q]:
+                        if j > first:
+                            copy(q, d, j - 1, first).wait_recv()
+                        copy(q, d, j, first).start()
+        for q in range(3):
+            for d in range(2):
+                for j in range(first, LATE[q]):
+                    copy(q, d, j, first).wait_send()
+                if LATE[q] > first:
+                    copy(q, d, LATE[q] - 1, first).wait_recv()
+
     ring.greet()
-    for j in range(max(LATE)):
-        for q in sorted(range(3), key=lambda q: -LATE[q]):
-            for d in range(2):
-                if j < LATE[q]:
-                    if j:
-                        copy(q, d, j - 1).wait_recv()
-                    copy(q, d, j).start()
-    for q in range(3):
-        for d in range(2):
-            for j in range(LATE[q]):
-                copy(q, d, j).wait_send()
-            copy(q, d, LATE[q] - 1).wait_recv()
+    pl.when(odd)(lambda: gather(1))
+    pl.when(jnp.logical_not(odd))(lambda: gather(0))
 
 
 def out_kernel(*refs):
@@ -219,20 +236,26 @@
     )(*arrays)
 
 
-def last_kernel(n, axis, *refs):
+def last_kernel(n, axis, groups, *refs):
     blocks, out, sem = refs[:3], refs[6:9], refs[9]
     ring = Ring(axis, n)
-    copies = []
-    for q in range(3):
-        rows = blocks[q].shape[2]
-        for d in range(2):
-            for j in range(LATE[q]):
-                there = out[q].at[d, pl.ds(ring.start_of(d, n - LATE[q] + j, rows), rows)]
-                copies.append(pltpu.make_async_copy(blocks[q].at[d, j], there, sem.at[q, d, j]))
-    for c in copies:
-        c.start()
-    for c in copies:
-        c.wait()
+    odd = is_odd(groups)
+
+    def write(first):
+        copies = []
+        for q in range(3):
+            rows = blocks[q].shape[2]
+            for d in range(2):
+                for j in range(first, LATE[q]):
+                    there = out[q].at[d, pl.ds(ring.start_of(d, n - LATE[q] + j, rows), rows)]
+                    copies.append(pltpu.make_async_copy(blocks[q].at[d, j], there, sem.at[q, d, j]))
+        for c in copies:
+            c.start()
+        for c in copies:
+            c.wait()
+
+    pl.when(odd)(lambda: write(1))
+    pl.when(jnp.logical_not(odd))(lambda: write(0))
 
 
 def solution(mesh):
@@ -267,7 +290,7 @@
         first = written(*results)
         gathered, first = lax.optimization_barrier((results[:3], first))
         blocks = pl.pallas_call(
-            functools.partial(second_kernel, n, axis),
+            functools.partial(second_kernel, n, axis, groups),
             out_shape=tuple(pltpu.VMEM((2, k, *s), BF16) for k, s in zip(LATE, shares, strict=True)),
             in_specs=[vmem] * 3,
             out_specs=tuple([vmem] * 3),
@@ -277,7 +300,7 @@
             ),
         )(*gathered)
         complete = pl.pallas_call(
-            functools.partial(last_kernel, n, axis),
+            functools.partial(last_kernel, n, axis, groups),
             out_shape=tuple(jax.ShapeDtypeStruct(w.shape, BF16) for w in weights),
             in_specs=[vmem] * 3 + [hbm] * 3,
             out_specs=tuple([hbm] * 3),

time: 367 us -> 366 us (level)
    pallas_call x2, Pallas kernels: 23.3 us -> 10.3 us  [the longest x1 9.3 us: step(): pl.pallas_call(functools.partial(second_kernel, n, axis, groups), out_sha...]
    pallas_call x1, Pallas kernels: 334 us -> 346 us  [step(): pl.pallas_call(functools.partial(first_kernel, n, axis, groups), out_shap...]
where the time goes in v2:
time: 366 us
  Pallas kernels  366 us (100%)
    pallas_call x1, Pallas kernels, step(): pl.pallas_call(functools.partial(first_kernel, n, axis, groups), out_shap...  346 us
    pallas_call x1, Pallas kernels, written(): pl.pallas_call(out_kernel, out_shape=tuple((jax.ShapeDtypeStruct(a.shape,...  9.45 us
    pallas_call x1, Pallas kernels, step(): pl.pallas_call(functools.partial(second_kernel, n, axis, groups), out_sha...  9.3 us

profile of v2, /device:TPU:21, one launch (start us, length us, event | category | flops | bytes accessed | tf_op | source)
XLA Modules:
  0.0 366.2 jit_solution(4899832791429561954)
XLA Ops:
  0.6 345.8 %shard_map.187 = (bf16[2,512,3072]{2,1,0:T(8,128)(2,1)S(1)}, bf16[2,512,3072]{2,1,0:T(8,128)(2,1)S(1)}, bf16[2,3072,512]{2,1,0:T(8,128)(2,1)S(1)}, f32[2,64,3072...) custom-call(bf16[2,512,3072]{2,1,0:T(8,128)(2,1)} %bitcast.3, ...), custom_call_target="tpu_custom_call" | custom-call | tf_op jit(solution)/shard_map/pallas_call | solution.py:273
  346.5 9.4 %shard_map.188 = (bf16[2,512,3072]{2,1,0:T(8,128)(2,1)}, bf16[2,512,3072]{2,1,0:T(8,128)(2,1)}, bf16[2,3072,512]{2,1,0:T(8,128)(2,1)}, f32[2,64,3072]{2,1,0:T(8,...) custom-call(bf16[2,512,3072]{2,1,0:T(8,128)(2,1)S(1)} %get-tuple-ele, ...), custom_call_target="tpu_custom_call" | custom-call | tf_op jit(solution)/shard_map/pallas_call | solution.py:229
  355.9 9.3 %shard_map.189 = (bf16[2,1,64,3072]{3,2,1,0:T(8,128)(2,1)S(1)}, bf16[2,1,64,3072]{3,2,1,0:T(8,128)(2,1)S(1)}, bf16[2,2,384,512]{3,2,1,0:T(8,128)(2,1)S(1)}) custom-call(bf16[2,512,3072]{2,1,0:T(8,128)(2,1)S(1)} %get-tuple-element.63.refs_0_, bf16[2,512,3072]{2,1,0:T(8,128)(2,1)S(1)} %get-tuple-element.64.refs_1_, ...), custom_call_target="tpu_custom_call" | custom-call | tf_op jit(solution)/shard_map/pallas_call | solution.py:292
  365.2 1.0 shard_map.190

commit v3 on v2

--- a/solution.py
+++ b/solution.py
@@ -12,7 +12,8 @@
 ROWS, COLS = 16, 512
 AHEAD = 3
 LATE = (1, 1, 2)
-LAG = 5000
+SHARE = 4
+LAG = 3000
 
 
 def adamw(w, m, v, g):
@@ -82,6 +83,11 @@
     def ag_copy(q, d, s):
         ref = w_out[q].at[d, block(d, s, q)]
         return ring.copy(d, ref, ref, ag_send.at[q, d, s], ag_recv.at[q, d, s])
+
+    def most_copy(d):
+        size = rows[2] - rows[2] // SHARE
+        ref = w_out[2].at[d, pl.ds(ring.start_of(d, last, rows[2]), size)]
+        return ring.copy(d, ref, ref, ag_send.at[2, d, last], ag_recv.at[2, d, last])
 
     def term_copy(q, d, s):
         slot = lax.rem(s, AHEAD)
@@ -181,8 +187,15 @@
 
     @pl.when(odd)
     def _():
-        for q, d in pairs:
-            ag_copy(q, d, steps[q]).wait()
+        for d in range(2):
+            ag_copy(2, d, steps[2]).wait_recv()
+            most_copy(d).start()
+        for q, d in pairs:
+            if q < 2:
+                ag_copy(q, d, steps[q]).wait_recv()
+            ag_copy(q, d, steps[q]).wait_send()
+        for d in range(2):
+            most_copy(d).wait()
 
 
 def second_kernel(n, axis, groups, *refs):
@@ -193,8 +206,11 @@
     def copy(q, d, j, first):
         rows = out[q].shape[2]
         hops = n - 1 - LATE[q] + j
-        src = w[q].at[d, pl.ds(ring.start_of(d, hops, rows), rows)] if j == first else out[q].at[d, j - 1]
-        return ring.copy(d, src, out[q].at[d, j], send.at[q, d, j], recv.at[q, d, j])
+        part = rows // SHARE if first else rows
+        here = pl.ds(rows - part, part)
+        there = pl.ds(pl.multiple_of(ring.start_of(d, hops, rows) + rows - part, ROWS), part)
+        src = w[q].at[d, there] if j == first else out[q].at[d, j - 1]
+        return ring.copy(d, src, out[q].at[d, j, here], send.at[q, d, j], recv.at[q, d, j])
 
     def gather(first):
         for j in range(first, max(LATE)):
@@ -247,8 +263,10 @@
             rows = blocks[q].shape[2]
             for d in range(2):
                 for j in range(first, LATE[q]):
-                    there = out[q].at[d, pl.ds(ring.start_of(d, n - LATE[q] + j, rows), rows)]
-                    copies.append(pltpu.make_async_copy(blocks[q].at[d, j], there, sem.at[q, d, j]))
+                    part = rows // SHARE if first else rows
+                    base = ring.start_of(d, n - LATE[q] + j, rows) + rows - part
+                    there = out[q].at[d, pl.ds(pl.multiple_of(base, ROWS), part)]
+                    copies.append(pltpu.make_async_copy(blocks[q].at[d, j, pl.ds(rows - part, part)], there, sem.at[q, d, j]))
         for c in copies:
             c.start()
         for c in copies:

time: 366 us -> 366 us (level)
    pallas_call x1, Pallas kernels: 346 us -> 350 us  [step(): pl.pallas_call(functools.partial(first_kernel, n, axis, groups), out_shap...]
    pallas_call x1, Pallas kernels: 9.3 us -> 4.98 us  [step(): pl.pallas_call(functools.partial(second_kernel, n, axis, groups), out_sha...]
where the time goes in v3:
time: 366 us
  Pallas kernels  365 us (100%)
    pallas_call x1, Pallas kernels, step(): pl.pallas_call(functools.partial(first_kernel, n, axis, groups), out_shap...  350 us
    pallas_call x1, Pallas kernels, written(): pl.pallas_call(out_kernel, out_shape=tuple((jax.ShapeDtypeStruct(a.shape,...  9.45 us

profile of v3, /device:TPU:21, one launch (start us, length us, event | category | flops | bytes accessed | tf_op | source)
XLA Modules:
  0.0 366.0 jit_solution(15580409760535164507)
XLA Ops:
  0.6 350.1 %shard_map.187 = (bf16[2,512,3072]{2,1,0:T(8,128)(2,1)S(1)}, bf16[2,512,3072]{2,1,0:T(8,128)(2,1)S(1)}, bf16[2,3072,512]{2,1,0:T(8,128)(2,1)S(1)}, f32[2,64,3072...) custom-call(bf16[2,512,3072]{2,1,0:T(8,128)(2,1)} %bitcast.3, ...), custom_call_target="tpu_custom_call" | custom-call | tf_op jit(solution)/shard_map/pallas_call | solution.py:291
  350.8 9.4 %shard_map.188 = (bf16[2,512,3072]{2,1,0:T(8,128)(2,1)}, bf16[2,512,3072]{2,1,0:T(8,128)(2,1)}, bf16[2,3072,512]{2,1,0:T(8,128)(2,1)}, f32[2,64,3072]{2,1,0:T(8,...) custom-call(bf16[2,512,3072]{2,1,0:T(8,128)(2,1)S(1)} %get-tuple-ele, ...), custom_call_target="tpu_custom_call" | custom-call | tf_op jit(solution)/shard_map/pallas_call | solution.py:245
  360.2 5.0 %shard_map.189 = (bf16[2,1,64,3072]{3,2,1,0:T(8,128)(2,1)S(1)}, bf16[2,1,64,3072]{3,2,1,0:T(8,128)(2,1)S(1)}, bf16[2,2,384,512]{3,2,1,0:T(8,128)(2,1)S(1)}) custom-call(bf16[2,512,3072]{2,1,0:T(8,128)(2,1)S(1)} %get-tuple-element.63.refs_0_, bf16[2,512,3072]{2,1,0:T(8,128)(2,1)S(1)} %get-tuple-element.64.refs_1_, ...), custom_call_target="tpu_custom_call" | custom-call | tf_op jit(solution)/shard_map/pallas_call | solution.py:310
  365.2 0.8 shard_map.190

commit v4 on v3

--- a/solution.py
+++ b/solution.py
@@ -12,8 +12,8 @@
 ROWS, COLS = 16, 512
 AHEAD = 3
 LATE = (1, 1, 2)
-SHARE = 4
-LAG = 3000
+SHARE = 24
+LAG = 2400
 
 
 def adamw(w, m, v, g):

time: 366 us -> 366 us (level)
  no operation moved by 1% of the time
where the time goes in v4:
time: 366 us
  Pallas kernels  366 us (100%)
    pallas_call x1, Pallas kernels, step(): pl.pallas_call(functools.partial(first_kernel, n, axis, groups), out_shap...  351 us
    pallas_call x1, Pallas kernels, written(): pl.pallas_call(out_kernel, out_shape=tuple((jax.ShapeDtypeStruct(a.shape,...  9.45 us

profile of v4, /device:TPU:21, one launch (start us, length us, event | category | flops | bytes accessed | tf_op | source)
XLA Modules:
  0.0 366.2 jit_solution(15598133813337684236)
XLA Ops:
  0.6 351.3 %shard_map.187 = (bf16[2,512,3072]{2,1,0:T(8,128)(2,1)S(1)}, bf16[2,512,3072]{2,1,0:T(8,128)(2,1)S(1)}, bf16[2,3072,512]{2,1,0:T(8,128)(2,1)S(1)}, f32[2,64,3072...) custom-call(bf16[2,512,3072]{2,1,0:T(8,128)(2,1)} %bitcast.3, ...), custom_call_target="tpu_custom_call" | custom-call | tf_op jit(solution)/shard_map/pallas_call | solution.py:291
  351.9 9.4 %shard_map.188 = (bf16[2,512,3072]{2,1,0:T(8,128)(2,1)}, bf16[2,512,3072]{2,1,0:T(8,128)(2,1)}, bf16[2,3072,512]{2,1,0:T(8,128)(2,1)}, f32[2,64,3072]{2,1,0:T(8,...) custom-call(bf16[2,512,3072]{2,1,0:T(8,128)(2,1)S(1)} %get-tuple-ele, ...), custom_call_target="tpu_custom_call" | custom-call | tf_op jit(solution)/shard_map/pallas_call | solution.py:245
  361.4 4.1 %shard_map.189 = (bf16[2,1,64,3072]{3,2,1,0:T(8,128)(2,1)S(1)}, bf16[2,1,64,3072]{3,2,1,0:T(8,128)(2,1)S(1)}, bf16[2,2,384,512]{3,2,1,0:T(8,128)(2,1)S(1)}) custom-call(bf16[2,512,3072]{2,1,0:T(8,128)(2,1)S(1)} %get-tuple-element.63.refs_0_, bf16[2,512,3072]{2,1,0:T(8,128)(2,1)S(1)} %get-tuple-element.64.refs_1_, ...), custom_call_target="tpu_custom_call" | custom-call | tf_op jit(solution)/shard_map/pallas_call | solution.py:310
  365.5 0.7 shard_map.190
